TPU v7x, 32 devices: a whole 2x2x4 slice. The times are simulated.
32 devices in a mesh: groups: 2 (over y), seq: 4 (over z), head: 2 (over x), layer: 2 (over core).
Axes of the slice: x: 2, y: 2, z: 4, core: 2. Of those that a mesh axis runs over, the one named last changes fastest.
Arguments:
- kv_cache: bfloat16 [2, 2, 8, 4096, 2, 128], P(None, 'layer', 'groups', 'seq', 'head'), parts along dimension 2, may hold values from -800 to 800
- valid_blocks: int32 [8], P('groups'), parts along dimension 0, may hold values from 1 to 32, 64 in all
Outputs:
- decode_cache: bfloat16 [2, 2, 8, 4096, 2, 128], P(None, 'layer', ('groups', 'seq'), None, 'head'), parts along dimension 2
- centers: float32 [2, 2, 8, 2, 128], P(None, 'layer', 'groups', 'head'), parts along dimension 2
- scales: float32 [2, 2, 8, 2, 128], P(None, 'layer', 'groups', 'head'), parts along dimension 2
There are 2 independent parts, one for each index of `groups`. A program takes and returns all parts, laid end to end along the dimension named above; each array names one. Nothing has to cross between parts.
Inputs may be any that keep to these rules, and one draw needn't show every extreme that they name: `valid_blocks`: the counts of the 4 users sum to 64, and the largest equals 32.
All inputs are finite; a program needn't handle non-finite values.
Results may differ from a plain program's by a relative error of at most 0.001.
Values may be sent and summed in bfloat16 or wider, within the bound.
A program may use at most 64 MiB of HBM per device.

v0:
```python
import jax
import jax.numpy as jnp
from jax import lax
from jax.sharding import PartitionSpec as P

BLOCK = 128


epsilon = 1e-06


def on_device(kv_cache, valid_blocks):
    kind_count, layer_dev, user_count, per_dev, heads_dev, head_dim = kv_cache.shape
    owners = lax.axis_size("seq")
    quarter = owners // user_count
    part_len = per_dev // quarter
    seq_index = lax.axis_index("seq")
    lengths = valid_blocks * BLOCK
    values = kv_cache.astype(jnp.float32)
    position = seq_index * per_dev + jnp.arange(per_dev, dtype=jnp.int32)
    is_live = position[None, :] < lengths[:, None]
    live_mask = is_live[None, None, :, :, None, None]
    local_sum = jnp.sum(jnp.where(live_mask, values, 0.0), axis=3)
    user_lengths = lengths.astype(jnp.float32)[None, None, :, None, None]
    totals = lax.psum(local_sum, "seq")
    centers = totals / user_lengths
    local_spread = jnp.max(
        jnp.where(live_mask, jnp.abs(values - centers[:, :, :, None]), 0.0), axis=3
    )
    spread = lax.pmax(local_spread, "seq")
    scales = spread + epsilon
    normed = jnp.where(
        live_mask, (values - centers[:, :, :, None]) / scales[:, :, :, None], 0.0
    ).astype(jnp.bfloat16)
    outgoing = normed.reshape(
        kind_count, layer_dev, user_count * quarter, part_len, heads_dev, head_dim
    )
    received = lax.all_to_all(outgoing, "seq", split_axis=2, concat_axis=2, tiled=True)
    arranged = received.reshape(kind_count, layer_dev, 1, owners * part_len, heads_dev, head_dim)
    return (arranged, centers, scales)


def solution(mesh):
    in_specs = (P(None, "layer", "groups", "seq", "head", None), P("groups"))
    out_specs = (
        P(None, "layer", ("groups", "seq"), None, "head", None),
        P(None, "layer", "groups", "head", None),
        P(None, "layer", "groups", "head", None),
    )
    return jax.shard_map(
        on_device, mesh=mesh, in_specs=in_specs, out_specs=out_specs, check_vma=False
    )
```

profile of v0, /device:TPU:0, one launch (start us, length us, event | category | flops | bytes accessed | tf_op | source)
XLA Modules:
  0.0 79.4 jit_solution(9776314781821777403)
XLA Ops:
  0.6 0.0 copy-start
  0.6 0.8 %fusion.7 = (f32[4]{0:T(128)S(1)}, s32[4]{0:T(128)S(1)}) fusion(s32[4]{0:T(128)} %param.3), kind=kLoop, calls=%fused_computation.14 | loop fusion | flops 8 | bytes 48 | tf_op jit(solution)/shard_map/convert_element_type | solution.py:24
  1.5 0.1 broadcast_compare_fusion
  1.5 2.8 %fusion.6 = f32[2,4,128]{2,0,1:T(2,128)S(1)} fusion(pred[4,1024]{1,0:T(4,128)(4,1)S(1)} %broadcast_compare_fusion, bf16[2,1,4,1024,1,128]{5,3,4,2,1,0:T(8,128)(2,1)} %param.2), kind=kLoop, calls=%fused_computation.8 | loop fusion | flops 3144704 | bytes 2105344 | tf_op jit(solution)/shard_map/reduce_sum | solution.py:23
  4.3 13.5 %psum.7 = f32[2,1,4,1,128]{4,0,2,3,1:T(2,128)S(1)} all-reduce(f32[2,1,4,1,128]{4,0,2,3,1:T(2,128)S(1)} %bitcast.10), channel_id=1, replica_groups=mesh['groups'=2,'seq'=4,'head'=2,'layer'=2] {'seq'}, use_global_device_ids=true, to_apply=%region_1.2 | all-reduce | flops 1024 | bytes 8192 | tf_op jit(solution)/shard_map/psum | solution.py:25
  17.8 0.1 fusion.9
  17.9 0.0 copy-done
  17.9 1.0 %fusion.3 = f32[2,4,128]{2,0,1:T(2,128)S(1)} fusion(f32[2,4,128]{2,0,1:T(2,128)S(1)} %fusion.9, pred[4,1024]{1,0:T(4,128)(4,1)S(1)} %broadcast_compare_fusion, bf16[2,1,4,1024,1,128]{5,3,4,2,1,0:T(8,128)(2,1)S(1)} %copy-done), kind=kLoop, calls=%fused_computation.5 | loop fusion | flops 5241856 | bytes 2109440 | tf_op jit(solution)/shard_map/reduce_max | solution.py:27
  18.9 8.4 %pmax.7 = f32[2,1,4,1,128]{4,0,2,3,1:T(2,128)S(1)} all-reduce(f32[2,1,4,1,128]{4,0,2,3,1:T(2,128)S(1)} %bitcast.11), channel_id=1, replica_groups=mesh['groups'=2,'seq'=4,'head'=2,'layer'=2] {'seq'}, use_global_device_ids=true, to_apply=%region_3.4 | all-reduce | flops 1024 | bytes 8192 | tf_op jit(solution)/shard_map/pmax | solution.py:30
  27.3 2.4 %fusion.5 = bf16[2,1,4,1024,1,128]{5,3,4,1,0,2:T(8,128)(2,1)} fusion(f32[2,4,128]{2,0,1:T(2,128)S(1)} %get-tuple-element.10, f32[2,4,128]{2,0,1:T(2,128)S(1)} %fusion.9, pred[4,1024]{1,0:T(4,128)(4,1)S(1)} %broadcast_compare_fusion, bf16[2,1,4,1024,1,128]{5,3,4,2,1,0:T(8,128)(2,1)S(1)} %copy-done), kind=kLoop, calls=%fused_computation.7 | loop fusion | flops 5242880 | bytes 4206592 | tf_op jit(solution)/shard_map/convert_element_type | solution.py:34
  29.7 3.6 %all-to-all-start = ((bf16[2,1,4,1024,1,128]{5,3,4,1,0,2:T(8,128)(2,1)}), bf16[2,1,4,1024,1,128]{5,3,4,1,0,2:T(8,128)(2,1)S(1)}, u32[]{:S(2)}, u32[]{:S(2)}) async-start(bf16[2,1,4,1024,1,128]{5,3,4,1,0,2:T(8,128)(2,1)} %fusion.5), calls=%async_computation | async-start | bytes 4194304 | tf_op jit(solution)/shard_map/all_to_all | solution.py:38
  33.3 0.1 broadcast_divide_fusion
  33.4 0.6 copy.16
  34.0 0.6 copy.17
  34.6 43.4 %all-to-all-done = bf16[2,1,4,1024,1,128]{5,3,4,1,0,2:T(8,128)(2,1)S(1)} async-done(((bf16[2,1,4,1024,1,128]{5,3,4,1,0,2:T(8,128)(2,1)}), bf16[2,1,4,1024,1,128]{5,3,4,1,0,2:T(8,128)(2,1)S(1)}, u32[]{:S(2)}, u32[]{:S(2)}) %all-to-all-start) | async-done | bytes 2097184 | tf_op jit(solution)/shard_map/all_to_all | solution.py:38
  77.9 1.5 %copy.14 = bf16[2,1,4,1024,1,128]{5,3,2,0,4,1:T(8,128)(2,1)} copy(bf16[2,1,4,1024,1,128]{5,3,4,1,0,2:T(8,128)(2,1)S(1)} %all-to-all-done) | data formatting | bytes 4194304 | tf_op jit(solution)/shard_map/all_to_all | solution.py:38
  (2 shorter events, 0.0 us)
Async XLA Ops:
  0.6 17.2 %copy-start = (bf16[2,1,4,1024,1,128]{5,3,4,2,1,0:T(8,128)(2,1)S(1)}, bf16[2,1,4,1024,1,128]{5,3,4,2,1,0:T(8,128)(2,1)}, u32[]{:S(2)}) copy-start(bf16[2,1,4,1024,1,128]{5,3,4,2,1,0:T(8,128)(2,1)} %param.2) | copy-start | bytes 6291460
  29.7 48.3 %all-to-all-start = ((bf16[2,1,4,1024,1,128]{5,3,4,1,0,2:T(8,128)(2,1)}), bf16[2,1,4,1024,1,128]{5,3,4,1,0,2:T(8,128)(2,1)S(1)}, u32[]{:S(2)}, u32[]{:S(2)}) async-start(bf16[2,1,4,1024,1,128]{5,3,4,1,0,2:T(8,128)(2,1)} %fusion.5), calls=%async_computation | async-start | bytes 4194304 | tf_op jit(solution)/shard_map/all_to_all | solution.py:38
where the time goes:
time: 79.7 us; the launch traced here: 79.4 us
  waiting for transfers between devices  43.4 us (54%)
  blocking collectives  21.9 us (27%)
  other arithmetic  7.21 us (9%)
  starting transfers between devices  3.61 us (5%)
  local copies, waits for them, and re-layouts  2.66 us (3%)
    all_to_all x1, waiting for transfers between devices, on_device(): lax.all_to_all(outgoing, 'seq', split_axis=2, concat_axis=2, tiled=True)  43.4 us
    psum x1, blocking collectives, on_device(): totals = lax.psum(local_sum, 'seq')  13.5 us
    pmax x1, blocking collectives, on_device(): spread = lax.pmax(local_spread, 'seq')  8.38 us
    all_to_all x1, starting transfers between devices, on_device(): lax.all_to_all(outgoing, 'seq', split_axis=2, concat_axis=2, tiled=True)  3.61 us
    reduce_sum x1, other arithmetic, on_device(): local_sum = jnp.sum(jnp.where(live_mask, values, 0.0), axis=3)  2.76 us
    convert_element_type x1, other arithmetic, on_device(): normed = jnp.where(live_mask, (values - centers[:, :, :, None]) / scales[...  2.37 us
  transfers between devices with their start and end apart: 1, of which 1 were waited for; matrix products, arithmetic and copies ran while one was open for 2% of the time, Pallas kernels for 0%

commit v1 on v0

v1 whole, which is shorter than its diff:
```python
import functools

import jax
import jax.numpy as jnp
from jax import lax
from jax.experimental import pallas as pl
from jax.experimental.pallas import tpu as pltpu
from jax.sharding import PartitionSpec as P

BLOCK = 128
ROWS = 8
GRANT = 16 * 2**20
EPSILON = 1e-06


def transport(n, quarter, blocks_ref, kv_ref, recv_ref, stats_ref, local, load_sem, own_sem,
              send_sem, recv_sem, stat_send, stat_recv):
    kinds, users, per_dev, width = kv_ref.shape
    part = per_dev // quarter
    me = lax.axis_index("seq")

    load = pltpu.make_async_copy(kv_ref, local, load_sem)
    load.start()

    barrier = pltpu.get_barrier_semaphore()
    for d in range(n):
        @pl.when(me != d)
        def _():
            pl.semaphore_signal(barrier, inc=1, device_id={"seq": d})
    pl.semaphore_wait(barrier, n - 1)

    def bulk(source, target, k):
        user, q = target // quarter, target % quarter
        return pltpu.make_async_remote_copy(
            src_ref=kv_ref.at[k, user, pl.ds(pl.multiple_of(q * part, part), part), :],
            dst_ref=recv_ref.at[k, pl.ds(pl.multiple_of(source * part, part), part), :],
            send_sem=send_sem.at[target, k],
            recv_sem=recv_sem.at[source, k],
            device_id={"seq": target},
        )

    def stat(source, target):
        return pltpu.make_async_remote_copy(
            src_ref=stats_ref.at[source],
            dst_ref=stats_ref.at[source],
            send_sem=stat_send.at[target],
            recv_sem=stat_recv.at[source],
            device_id={"seq": target},
        )

    def start_bulk(dist):
        for k in range(kinds):
            @pl.when(me + dist < n)
            def _():
                bulk(me, me + dist, k).start()

            @pl.when(me - dist >= 0)
            def _():
                bulk(me, me - dist, k).start()

    start_bulk(1)
    own = pltpu.make_async_copy(
        kv_ref.at[:, me // quarter, pl.ds(pl.multiple_of((me % quarter) * part, part), part), :],
        recv_ref.at[:, pl.ds(pl.multiple_of(me * part, part), part), :],
        own_sem,
    )
    own.start()
    load.wait()

    count = per_dev // BLOCK
    for k in range(kinds):
        for u in range(users):
            live = blocks_ref[u] - me * count

            def step(b, carry, k=k, u=u, live=live):
                total, high, low = carry
                x = local[k, u, pl.ds(pl.multiple_of(b * BLOCK, BLOCK), BLOCK), :].astype(jnp.float32)
                x = x.reshape(BLOCK // ROWS, ROWS, width)
                on = b < live
                total = total + jnp.where(on, jnp.sum(x, axis=0), 0.0)
                high = jnp.maximum(high, jnp.where(on, jnp.max(x, axis=0), -jnp.inf))
                low = jnp.minimum(low, jnp.where(on, jnp.min(x, axis=0), jnp.inf))
                return total, high, low

            shape = (ROWS, width)
            total, high, low = lax.fori_loop(
                0, count, step,
                (jnp.zeros(shape, jnp.float32), jnp.full(shape, -jnp.inf, jnp.float32),
                 jnp.full(shape, jnp.inf, jnp.float32)),
            )
            stats_ref[me, 0, k, u, :] = jnp.sum(total, axis=0)
            stats_ref[me, 1, k, u, :] = jnp.max(high, axis=0)
            stats_ref[me, 2, k, u, :] = jnp.min(low, axis=0)

    for d in range(n):
        @pl.when(me != d)
        def _():
            stat(me, d).start()
    for dist in range(2, n):
        start_bulk(dist)

    own.wait()
    for s in range(n):
        @pl.when(me != s)
        def _():
            stat(me, s).wait_send()
            stat(s, me).wait_recv()
            for k in range(kinds):
                bulk(me, s, k).wait_send()
                bulk(s, me, k).wait_recv()


def finish(n, quarter, chunk, blocks_ref, recv_ref, stats_ref, out_ref, centers_ref, scales_ref,
           inverse, ready, out_sem):
    _, _, kinds, users, width = stats_ref.shape
    positions = recv_ref.shape[1]
    part = positions // n
    me = lax.axis_index("seq")
    for u in range(users):
        length = (blocks_ref[u] * BLOCK).astype(jnp.float32)
        for k in range(kinds):
            total = stats_ref[0, 0, k, u, :]
            high, low = stats_ref[0, 1, k, u, :], stats_ref[0, 2, k, u, :]
            for s in range(1, n):
                total = total + stats_ref[s, 0, k, u, :]
                high = jnp.maximum(high, stats_ref[s, 1, k, u, :])
                low = jnp.minimum(low, stats_ref[s, 2, k, u, :])
            center = total / jnp.full_like(total, length)
            scale = jnp.maximum(high - center, center - low) + EPSILON
            centers_ref[k, u, :] = center
            scales_ref[k, u, :] = scale
            inverse[k, u, :] = 1.0 / scale

    user = me // quarter
    length = blocks_ref[user] * BLOCK
    per_part = part // chunk
    per_dev = part * quarter
    base = (me % quarter) * part
    iota = lax.broadcasted_iota(jnp.int32, (chunk, width), 0)
    for k in range(kinds):
        center = centers_ref[k, pl.ds(user, 1), :]
        scale = inverse[k, pl.ds(user, 1), :]

        def step(i, _, k=k, center=center, scale=scale):
            rows = pl.ds(pl.multiple_of(i * chunk, chunk), chunk)
            first = (i // per_part) * per_dev + base + (i % per_part) * chunk
            x = recv_ref[k, rows, :].astype(jnp.float32)
            y = jnp.where(first + iota < length, (x - center) * scale, 0.0)
            ready[k, rows, :] = y.astype(jnp.bfloat16)
            pltpu.make_async_copy(ready.at[k, rows, :], out_ref.at[k, rows, :],
                                  out_sem.at[k, i]).start()
            return 0

        lax.fori_loop(0, positions // chunk, step, 0)
    for k in range(kinds):
        def done(i, _, k=k):
            rows = pl.ds(pl.multiple_of(i * chunk, chunk), chunk)
            pltpu.make_async_copy(ready.at[k, rows, :], out_ref.at[k, rows, :],
                                  out_sem.at[k, i]).wait()
            return 0

        lax.fori_loop(0, positions // chunk, done, 0)


def on_device(kv_cache, valid_blocks):
    kind_count, layer_dev, user_count, per_dev, heads_dev, width = kv_cache.shape
    n = lax.axis_size("seq")
    quarter = n // user_count
    part = per_dev // quarter
    kinds = kind_count * layer_dev * heads_dev
    kv = jnp.transpose(kv_cache, (0, 1, 4, 2, 3, 5)).reshape(kinds, user_count, per_dev, width)
    vmem = pl.BlockSpec(memory_space=pltpu.VMEM)
    smem = pl.BlockSpec(memory_space=pltpu.SMEM)
    anywhere = pl.BlockSpec(memory_space=pl.ANY)
    recv, stats = pl.pallas_call(
        functools.partial(transport, n, quarter),
        out_shape=(
            jax.ShapeDtypeStruct((kinds, n * part, width), jnp.bfloat16),
            jax.ShapeDtypeStruct((n, 3, kinds, user_count, width), jnp.float32),
        ),
        in_specs=[smem, anywhere],
        out_specs=(vmem, vmem),
        scratch_shapes=[
            pltpu.VMEM((kinds, user_count, per_dev, width), jnp.bfloat16),
            pltpu.SemaphoreType.DMA,
            pltpu.SemaphoreType.DMA,
            pltpu.SemaphoreType.DMA((n, kinds)),
            pltpu.SemaphoreType.DMA((n, kinds)),
            pltpu.SemaphoreType.DMA((n,)),
            pltpu.SemaphoreType.DMA((n,)),
        ],
        compiler_params=pltpu.CompilerParams(
            collective_id=0, has_side_effects=True, vmem_limit_bytes=GRANT
        ),
        name="transport",
    )(valid_blocks, kv)
    chunk = min(part, 512)
    small = jax.ShapeDtypeStruct((kinds, user_count, width), jnp.float32)
    out, centers, scales = pl.pallas_call(
        functools.partial(finish, n, quarter, chunk),
        out_shape=(jax.ShapeDtypeStruct((kinds, n * part, width), jnp.bfloat16), small, small),
        in_specs=[smem, vmem, vmem],
        out_specs=(anywhere, vmem, vmem),
        scratch_shapes=[
            pltpu.VMEM((kinds, user_count, width), jnp.float32),
            pltpu.VMEM((kinds, n * part, width), jnp.bfloat16),
            pltpu.SemaphoreType.DMA((kinds, n * part // chunk)),
        ],
        compiler_params=pltpu.CompilerParams(vmem_limit_bytes=GRANT),
        name="finish",
    )(valid_blocks, recv, stats)

    def spread(x, middle):
        x = x.reshape(kind_count, layer_dev, heads_dev, *middle, width)
        return jnp.moveaxis(x, 2, -2)

    return (
        spread(out, (1, n * part)),
        spread(centers, (user_count,)),
        spread(scales, (user_count,)),
    )


def solution(mesh):
    in_specs = (P(None, "layer", "groups", "seq", "head", None), P("groups"))
    out_specs = (
        P(None, "layer", ("groups", "seq"), None, "head", None),
        P(None, "layer", "groups", "head", None),
        P(None, "layer", "groups", "head", None),
    )
    return jax.shard_map(
        on_device, mesh=mesh, in_specs=in_specs, out_specs=out_specs, check_vma=False
    )
```

time: 79.7 us -> 59.1 us (0.74)
  Pallas kernels: 0 us -> 56.1 us
  waiting for transfers between devices: 43.4 us -> 0 us
  blocking collectives: 21.9 us -> 0 us
  other arithmetic: 7.21 us -> 0 us
  starting transfers between devices: 3.61 us -> 0 us
    pallas_call x0 -> x2, Pallas kernels: none -> 56.1 us  [the longest x1 53 us: on_device(): pl.pallas_call(functools.partial(transport, n, quarter), out_shape=(jax.S...]
    all_to_all x1 -> x0, waiting for transfers between devices: 43.4 us -> none  [on_device(): lax.all_to_all(outgoing, 'seq', split_axis=2, concat_axis=2, tiled=True)]
    psum x1 -> x0, blocking collectives: 13.5 us -> none  [on_device(): totals = lax.psum(local_sum, 'seq')]
    pmax x1 -> x0, blocking collectives: 8.38 us -> none  [on_device(): spread = lax.pmax(local_spread, 'seq')]
    all_to_all x1 -> x0, starting transfers between devices: 3.61 us -> none  [on_device(): lax.all_to_all(outgoing, 'seq', split_axis=2, concat_axis=2, tiled=True)]
    convert_element_type x2 -> x0, other arithmetic: 3.17 us -> none  [the longest x1 2.37 us: on_device(): normed = jnp.where(live_mask, (values - centers[:, :, :, None]) / scales[...]
    reduce_sum x1 -> x0, other arithmetic: 2.76 us -> none  [on_device(): local_sum = jnp.sum(jnp.where(live_mask, values, 0.0), axis=3)]
    all_to_all x1 -> x0, local copies, waits for them, and re-layouts: 1.45 us -> none  [on_device(): lax.all_to_all(outgoing, 'seq', split_axis=2, concat_axis=2, tiled=True)]
  transfers between devices with their start and end apart: 1 -> 0, of which waited for: 1 -> 0; matrix products, arithmetic and copies ran while one was open for 2% -> 0% of each run, Pallas kernels for 0% -> 0%
where the time goes in v1:
time: 59.1 us; the launch traced here: 59 us
  Pallas kernels  56.1 us (95%)
  local copies, waits for them, and re-layouts  2.24 us (4%)
  between operations  0.65 us (1%)
    pallas_call x1, Pallas kernels, on_device(): pl.pallas_call(functools.partial(transport, n, quarter), out_shape=(jax.S...  53 us
    pallas_call x1, Pallas kernels, on_device(): pl.pallas_call(functools.partial(finish, n, quarter, chunk), out_shape=(j...  3.05 us
    unnamed x4, local copies, waits for them, and re-layouts  2.24 us

profile of v1, /device:TPU:0, one launch (start us, length us, event | category | flops | bytes accessed | tf_op | source)
XLA Modules:
  0.0 59.0 jit_solution(13170366238392065047)
XLA Ops:
  0.6 0.0 copy-start
  0.6 1.6 %copy-done = bf16[2,1,4,1024,1,128]{5,3,4,2,1,0:T(8,128)(2,1)S(1)} copy-done((bf16[2,1,4,1024,1,128]{5,3,4,2,1,0:T(8,128)(2,1)S(1)}, bf16[2,1,4,1024,1,128]{5,3,4,2,1,0:T(8,128)(2,1)}, u32[]{:S(2)}) %copy-start) | copy-done | bytes 2097176
  2.2 0.0 copy-start.1
  2.2 0.7 %copy-done.1 = s32[4]{0:T(128)S(1)} copy-done((s32[4]{0:T(128)S(1)}, s32[4]{0:T(128)}, u32[]{:S(2)}) %copy-start.1) | copy-done | bytes 40
  2.9 53.0 %transport.1 = (bf16[2,4096,128]{2,1,0:T(8,128)(2,1)S(1)}, f32[4,3,2,4,128]{4,3,2,1,0:T(4,128)S(1)}) custom-call(s32[4]{0:T(128)S(1)} %copy-done.1, bf16[2,4,1024,128]{3,2,1,0:T(8,128)(2,1)S(1)} %bitcast.10), custom_call_target="tpu_custom_call" | custom-call | tf_op jit(solution)/shard_map/transport/pallas_call | solution.py:175
  55.9 3.1 %finish.1 = (bf16[2,4096,128]{2,1,0:T(8,128)(2,1)}, f32[2,4,128]{2,1,0:T(4,128)}, f32[2,4,128]{2,1,0:T(4,128)}) custom-call(s32[4]{0:T(128)S(1)} %copy-done.1, bf16[2,4096,128]{2,1,0:T(8,128)(2,1)S(1)} %get-tuple-element.8.recv_ref, f32[4,3,2,4,128]{4,3,2,1,0:T(4,128)S(1)} %get-tuple-element.9.stats_ref), custom_call_target="tpu_custom_call" | custom-call | tf_op jit(solution)/shard_map/finish/pallas_call | solution.py:199
Async XLA Ops:
  0.6 1.6 %copy-start = (bf16[2,1,4,1024,1,128]{5,3,4,2,1,0:T(8,128)(2,1)S(1)}, bf16[2,1,4,1024,1,128]{5,3,4,2,1,0:T(8,128)(2,1)}, u32[]{:S(2)}) copy-start(bf16[2,1,4,1024,1,128]{5,3,4,2,1,0:T(8,128)(2,1)} %param.2) | copy-start | bytes 6291460
  2.2 0.7 %copy-start.1 = (s32[4]{0:T(128)S(1)}, s32[4]{0:T(128)}, u32[]{:S(2)}) copy-start(s32[4]{0:T(128)} %blocks_ref.3) | copy-start | bytes 52

commit v2 on v1

--- a/solution.py
+++ b/solution.py
@@ -9,18 +9,32 @@
 
 BLOCK = 128
 ROWS = 8
+CHUNK = 256
 GRANT = 16 * 2**20
 EPSILON = 1e-06
 
 
-def transport(n, quarter, blocks_ref, kv_ref, recv_ref, stats_ref, local, load_sem, own_sem,
-              send_sem, recv_sem, stat_send, stat_recv):
+def normalised(recv_ref, k, rows, first, length, center, inverse):
+    x = recv_ref[k, rows, :].astype(jnp.float32)
+    position = first + lax.broadcasted_iota(jnp.int32, x.shape, 0)
+    return jnp.where(position < length, (x - center) * inverse, 0.0).astype(jnp.bfloat16)
+
+
+def last_source(me, n):
+    return jnp.where(me < n - 1 - me, n - 1, 0)
+
+
+def transport(n, quarter, chunk, blocks_ref, kv_ref, recv_ref, stats_ref, centers_ref, scales_ref,
+              inverse_ref, blocks, local, load_sem, blocks_sem, own_sem, send_sem, recv_sem,
+              stat_send, stat_recv):
     kinds, users, per_dev, width = kv_ref.shape
     part = per_dev // quarter
     me = lax.axis_index("seq")
 
     load = pltpu.make_async_copy(kv_ref, local, load_sem)
     load.start()
+    fetch = pltpu.make_async_copy(blocks_ref, blocks, blocks_sem)
+    fetch.start()
 
     barrier = pltpu.get_barrier_semaphore()
     for d in range(n):
@@ -65,12 +79,13 @@
         own_sem,
     )
     own.start()
+    fetch.wait()
     load.wait()
 
     count = per_dev // BLOCK
     for k in range(kinds):
         for u in range(users):
-            live = blocks_ref[u] - me * count
+            live = blocks[u] - me * count
 
             def step(b, carry, k=k, u=u, live=live):
                 total, high, low = carry
@@ -99,25 +114,12 @@
     for dist in range(2, n):
         start_bulk(dist)
 
-    own.wait()
     for s in range(n):
         @pl.when(me != s)
         def _():
-            stat(me, s).wait_send()
             stat(s, me).wait_recv()
-            for k in range(kinds):
-                bulk(me, s, k).wait_send()
-                bulk(s, me, k).wait_recv()
-
-
-def finish(n, quarter, chunk, blocks_ref, recv_ref, stats_ref, out_ref, centers_ref, scales_ref,
-           inverse, ready, out_sem):
-    _, _, kinds, users, width = stats_ref.shape
-    positions = recv_ref.shape[1]
-    part = positions // n
-    me = lax.axis_index("seq")
     for u in range(users):
-        length = (blocks_ref[u] * BLOCK).astype(jnp.float32)
+        length = (blocks[u] * BLOCK).astype(jnp.float32)
         for k in range(kinds):
             total = stats_ref[0, 0, k, u, :]
             high, low = stats_ref[0, 1, k, u, :], stats_ref[0, 2, k, u, :]
@@ -129,37 +131,96 @@
             scale = jnp.maximum(high - center, center - low) + EPSILON
             centers_ref[k, u, :] = center
             scales_ref[k, u, :] = scale
-            inverse[k, u, :] = 1.0 / scale
+            inverse_ref[k, u, :] = 1.0 / scale
+
+    user = me // quarter
+    base = (me % quarter) * part
+    length = jnp.zeros((1, width), jnp.int32)
+    for u in range(users):
+        length = jnp.where(user == u, blocks[u] * BLOCK, length)
+
+    def normalise(source, k):
+        center = centers_ref[k, pl.ds(user, 1), :]
+        inverse = inverse_ref[k, pl.ds(user, 1), :]
+
+        def step(i, _):
+            rows = pl.ds(pl.multiple_of(source * part + i * chunk, chunk), chunk)
+            first = source * per_dev + base + i * chunk
+            recv_ref[k, rows, :] = normalised(recv_ref, k, rows, first, length, center, inverse)
+            return 0
+
+        lax.fori_loop(0, part // chunk, step, 0)
+
+    own.wait()
+    for k in range(kinds):
+        normalise(me, k)
+    last = last_source(me, n)
+    for dist in range(1, n):
+        for source, inside in ((me + dist, me + dist < n), (me - dist, me - dist >= 0)):
+            for k in range(kinds):
+                @pl.when(inside & (source != last))
+                def _():
+                    bulk(source, me, k).wait_recv()
+                    normalise(source, k)
+    for k in range(kinds):
+        bulk(last, me, k).wait_recv()
+    for s in range(n):
+        @pl.when(me != s)
+        def _():
+            stat(me, s).wait_send()
+            for k in range(kinds):
+                bulk(me, s, k).wait_send()
+
+
+def finish(n, quarter, chunk, blocks_ref, recv_ref, c_ref, s_ref, i_ref, out_ref, centers_ref,
+           scales_ref, ready, out_sem, ready_sem):
+    kinds, positions, width = recv_ref.shape
+    part = positions // n
+    me = lax.axis_index("seq")
+    last = last_source(me, n)
+
+    def place(s, k):
+        rows = pl.ds(pl.multiple_of(s * part, part), part)
+        return pltpu.make_async_copy(recv_ref.at[k, rows, :], out_ref.at[k, rows, :],
+                                     out_sem.at[s, k])
+
+    for s in range(n):
+        @pl.when(s != last)
+        def _():
+            for k in range(kinds):
+                place(s, k).start()
 
     user = me // quarter
     length = blocks_ref[user] * BLOCK
-    per_part = part // chunk
-    per_dev = part * quarter
-    base = (me % quarter) * part
-    iota = lax.broadcasted_iota(jnp.int32, (chunk, width), 0)
-    for k in range(kinds):
-        center = centers_ref[k, pl.ds(user, 1), :]
-        scale = inverse[k, pl.ds(user, 1), :]
-
-        def step(i, _, k=k, center=center, scale=scale):
-            rows = pl.ds(pl.multiple_of(i * chunk, chunk), chunk)
-            first = (i // per_part) * per_dev + base + (i % per_part) * chunk
-            x = recv_ref[k, rows, :].astype(jnp.float32)
-            y = jnp.where(first + iota < length, (x - center) * scale, 0.0)
-            ready[k, rows, :] = y.astype(jnp.bfloat16)
-            pltpu.make_async_copy(ready.at[k, rows, :], out_ref.at[k, rows, :],
-                                  out_sem.at[k, i]).start()
-            return 0
-
-        lax.fori_loop(0, positions // chunk, step, 0)
-    for k in range(kinds):
-        def done(i, _, k=k):
-            rows = pl.ds(pl.multiple_of(i * chunk, chunk), chunk)
-            pltpu.make_async_copy(ready.at[k, rows, :], out_ref.at[k, rows, :],
-                                  out_sem.at[k, i]).wait()
-            return 0
-
-        lax.fori_loop(0, positions // chunk, done, 0)
+    first = last * part * quarter + (me % quarter) * part
+    steps = part // chunk
+
+    def late(k, i):
+        return pltpu.make_async_copy(
+            ready.at[k, pl.ds(i * chunk, chunk), :],
+            out_ref.at[k, pl.ds(pl.multiple_of(last * part + i * chunk, chunk), chunk), :],
+            ready_sem.at[k, i],
+        )
+
+    for k in range(kinds):
+        center = c_ref[k, pl.ds(user, 1), :]
+        inverse = i_ref[k, pl.ds(user, 1), :]
+        for i in range(steps):
+            rows = pl.ds(pl.multiple_of(last * part + i * chunk, chunk), chunk)
+            ready[k, pl.ds(i * chunk, chunk), :] = normalised(
+                recv_ref, k, rows, first + i * chunk, length, center, inverse
+            )
+            late(k, i).start()
+    centers_ref[...] = c_ref[...]
+    scales_ref[...] = s_ref[...]
+    for k in range(kinds):
+        for i in range(steps):
+            late(k, i).wait()
+    for s in range(n):
+        @pl.when(s != last)
+        def _():
+            for k in range(kinds):
+                place(s, k).wait()
 
 
 def on_device(kv_cache, valid_blocks):
@@ -169,19 +230,29 @@
     part = per_dev // quarter
     kinds = kind_count * layer_dev * heads_dev
     kv = jnp.transpose(kv_cache, (0, 1, 4, 2, 3, 5)).reshape(kinds, user_count, per_dev, width)
+    kv = pltpu.with_memory_space_constraint(kv, pltpu.HBM)
+    blocks = pltpu.with_memory_space_constraint(valid_blocks, pltpu.HBM)
     vmem = pl.BlockSpec(memory_space=pltpu.VMEM)
     smem = pl.BlockSpec(memory_space=pltpu.SMEM)
     anywhere = pl.BlockSpec(memory_space=pl.ANY)
-    recv, stats = pl.pallas_call(
-        functools.partial(transport, n, quarter),
+    hbm = pl.BlockSpec(memory_space=pltpu.HBM)
+    chunk = min(part, CHUNK)
+    small = jax.ShapeDtypeStruct((kinds, user_count, width), jnp.float32)
+    recv, _, centers, scales, inverse = pl.pallas_call(
+        functools.partial(transport, n, quarter, chunk),
         out_shape=(
             jax.ShapeDtypeStruct((kinds, n * part, width), jnp.bfloat16),
             jax.ShapeDtypeStruct((n, 3, kinds, user_count, width), jnp.float32),
+            small,
+            small,
+            small,
         ),
-        in_specs=[smem, anywhere],
-        out_specs=(vmem, vmem),
+        in_specs=[hbm, hbm],
+        out_specs=(vmem,) * 5,
         scratch_shapes=[
+            pltpu.SMEM((user_count,), jnp.int32),
             pltpu.VMEM((kinds, user_count, per_dev, width), jnp.bfloat16),
+            pltpu.SemaphoreType.DMA,
             pltpu.SemaphoreType.DMA,
             pltpu.SemaphoreType.DMA,
             pltpu.SemaphoreType.DMA((n, kinds)),
@@ -193,22 +264,20 @@
             collective_id=0, has_side_effects=True, vmem_limit_bytes=GRANT
         ),
         name="transport",
-    )(valid_blocks, kv)
-    chunk = min(part, 512)
-    small = jax.ShapeDtypeStruct((kinds, user_count, width), jnp.float32)
+    )(blocks, kv)
     out, centers, scales = pl.pallas_call(
         functools.partial(finish, n, quarter, chunk),
         out_shape=(jax.ShapeDtypeStruct((kinds, n * part, width), jnp.bfloat16), small, small),
-        in_specs=[smem, vmem, vmem],
+        in_specs=[smem, vmem, vmem, vmem, vmem],
         out_specs=(anywhere, vmem, vmem),
         scratch_shapes=[
-            pltpu.VMEM((kinds, user_count, width), jnp.float32),
-            pltpu.VMEM((kinds, n * part, width), jnp.bfloat16),
-            pltpu.SemaphoreType.DMA((kinds, n * part // chunk)),
+            pltpu.VMEM((kinds, part, width), jnp.bfloat16),
+            pltpu.SemaphoreType.DMA((n, kinds)),
+            pltpu.SemaphoreType.DMA((kinds, part // chunk)),
         ],
         compiler_params=pltpu.CompilerParams(vmem_limit_bytes=GRANT),
         name="finish",
-    )(valid_blocks, recv, stats)
+    )(valid_blocks, recv, centers, scales, inverse)
 
     def spread(x, middle):
         x = x.reshape(kind_count, layer_dev, heads_dev, *middle, width)

time: 59.1 us -> 56.7 us (0.959)
  local copies, waits for them, and re-layouts: 2.24 us -> 0.01 us
    unnamed x4 -> x2, local copies, waits for them, and re-layouts: 2.24 us -> 0.01 us
where the time goes in v2:
time: 56.7 us; the launch traced here: 56.6 us
  Pallas kernels  55.9 us (99%)
  between operations  0.65 us (1%)
    pallas_call x1, Pallas kernels, on_device(): pl.pallas_call(functools.partial(transport, n, quarter, chunk), out_shape...  53.3 us
    pallas_call x1, Pallas kernels, on_device(): pl.pallas_call(functools.partial(finish, n, quarter, chunk), out_shape=(j...  2.59 us

profile of v2, /device:TPU:0, one launch (start us, length us, event | category | flops | bytes accessed | tf_op | source)
XLA Modules:
  0.0 56.6 jit_solution(7732924484079266087)
XLA Ops:
  0.6 0.0 copy-start
  0.6 53.3 %transport.1 = (bf16[2,4096,128]{2,1,0:T(8,128)(2,1)S(1)}, f32[4,3,2,4,128]{4,3,2,1,0:T(4,128)}, f32[2,4,128]{2,1,0:T(4,128)S(1)}, f32[2,4,128]{2,1,0:T(4,128)S(1)}, f32[2,4,128]{2,1,0:T(4,128)S(1)}) custom-call(s32[4]{0:T(128)} %blocks_ref.3, bf16[2,4,1024,128]{3,2,1,0:T(8,128)(2,1)} %bitcast.10), custom_call_target="tpu_custom_call" | custom-call | tf_op jit(solution)/shard_map/transport/pallas_call | solution.py:241
  54.0 0.0 copy-done
  54.0 2.6 %finish.1 = (bf16[2,4096,128]{2,1,0:T(8,128)(2,1)}, f32[2,4,128]{2,1,0:T(4,128)}, f32[2,4,128]{2,1,0:T(4,128)}) custom-call(s32[4]{0:T(128)S(1)} %copy-done, bf16[2,4096,128]{2,1,0:T(8,128)(2,1)S(1)} %get-tuple-element.10.recv_ref, f32[2,4,128]{2,1,0:T(4,128)S(1)} %get-tuple-element.11.c_ref, f32[2,4,128]{2,1,0:T(4,128)S(1)} %get-tuple-element.12.s_ref, ...), custom_call_target="tpu_custom_call" | custom-call | tf_op jit(solution)/shard_map/finish/pallas_call | solution.py:268
Async XLA Ops:
  0.6 53.4 %copy-start = (s32[4]{0:T(128)S(1)}, s32[4]{0:T(128)}, u32[]{:S(2)}) copy-start(s32[4]{0:T(128)} %blocks_ref.3) | copy-start | bytes 52

commit v3 on v2

--- a/solution.py
+++ b/solution.py
@@ -26,7 +26,7 @@
 
 def transport(n, quarter, chunk, blocks_ref, kv_ref, recv_ref, stats_ref, centers_ref, scales_ref,
               inverse_ref, blocks, local, load_sem, blocks_sem, own_sem, send_sem, recv_sem,
-              stat_send, stat_recv):
+              stat_send, stat_recv, entered):
     kinds, users, per_dev, width = kv_ref.shape
     part = per_dev // quarter
     me = lax.axis_index("seq")
@@ -37,16 +37,22 @@
     fetch.start()
 
     barrier = pltpu.get_barrier_semaphore()
-    for d in range(n):
-        @pl.when(me != d)
-        def _():
-            pl.semaphore_signal(barrier, inc=1, device_id={"seq": d})
-    pl.semaphore_wait(barrier, n - 1)
-
-    def bulk(source, target, k):
+    has_right, has_left = me + 1 < n, me >= 1
+
+    @pl.when(has_right)
+    def _():
+        pl.semaphore_signal(barrier, inc=1, device_id={"seq": me + 1})
+
+    @pl.when(has_left)
+    def _():
+        pl.semaphore_signal(barrier, inc=1, device_id={"seq": me - 1})
+
+    pl.semaphore_wait(barrier, has_right.astype(jnp.int32) + has_left.astype(jnp.int32))
+
+    def bulk(source, target, k, origin=kv_ref):
         user, q = target // quarter, target % quarter
         return pltpu.make_async_remote_copy(
-            src_ref=kv_ref.at[k, user, pl.ds(pl.multiple_of(q * part, part), part), :],
+            src_ref=origin.at[k, user, pl.ds(pl.multiple_of(q * part, part), part), :],
             dst_ref=recv_ref.at[k, pl.ds(pl.multiple_of(source * part, part), part), :],
             send_sem=send_sem.at[target, k],
             recv_sem=recv_sem.at[source, k],
@@ -62,23 +68,41 @@
             device_id={"seq": target},
         )
 
-    def start_bulk(dist):
+    def start_bulk(dist, origin):
         for k in range(kinds):
             @pl.when(me + dist < n)
             def _():
-                bulk(me, me + dist, k).start()
+                bulk(me, me + dist, k, origin).start()
 
             @pl.when(me - dist >= 0)
             def _():
-                bulk(me, me - dist, k).start()
-
-    start_bulk(1)
+                bulk(me, me - dist, k, origin).start()
+
+    start_bulk(1, kv_ref)
     own = pltpu.make_async_copy(
         kv_ref.at[:, me // quarter, pl.ds(pl.multiple_of((me % quarter) * part, part), part), :],
         recv_ref.at[:, pl.ds(pl.multiple_of(me * part, part), part), :],
         own_sem,
     )
     own.start()
+
+    for dist in range(2, n):
+        @pl.when(has_right & (me - (dist - 1) >= 0))
+        def _():
+            pl.semaphore_signal(entered.at[0, dist], inc=1, device_id={"seq": me + 1})
+
+        @pl.when(has_left & (me + (dist - 1) < n))
+        def _():
+            pl.semaphore_signal(entered.at[1, dist], inc=1, device_id={"seq": me - 1})
+
+        @pl.when(me - dist >= 0)
+        def _():
+            pl.semaphore_wait(entered.at[0, dist], 1)
+
+        @pl.when(me + dist < n)
+        def _():
+            pl.semaphore_wait(entered.at[1, dist], 1)
+
     fetch.wait()
     load.wait()
 
@@ -111,8 +135,8 @@
         @pl.when(me != d)
         def _():
             stat(me, d).start()
-    for dist in range(2, n):
-        start_bulk(dist)
+    for dist in range(n - 1, 1, -1):
+        start_bulk(dist, local)
 
     for s in range(n):
         @pl.when(me != s)
@@ -155,7 +179,7 @@
     for k in range(kinds):
         normalise(me, k)
     last = last_source(me, n)
-    for dist in range(1, n):
+    for dist in (1, *range(n - 1, 1, -1)):
         for source, inside in ((me + dist, me + dist < n), (me - dist, me - dist >= 0)):
             for k in range(kinds):
                 @pl.when(inside & (source != last))
@@ -259,6 +283,7 @@
             pltpu.SemaphoreType.DMA((n, kinds)),
             pltpu.SemaphoreType.DMA((n,)),
             pltpu.SemaphoreType.DMA((n,)),
+            pltpu.SemaphoreType.REGULAR((2, n)),
         ],
         compiler_params=pltpu.CompilerParams(
             collective_id=0, has_side_effects=True, vmem_limit_bytes=GRANT

time: 56.7 us -> 56.8 us (level)
  no operation moved by 1% of the time
where the time goes in v3:
time: 56.8 us; the launch traced here: 56.6 us
  Pallas kernels  56 us (99%)
  between operations  0.65 us (1%)
    pallas_call x1, Pallas kernels, on_device(): pl.pallas_call(functools.partial(transport, n, quarter, chunk), out_shape...  53.4 us
    pallas_call x1, Pallas kernels, on_device(): pl.pallas_call(functools.partial(finish, n, quarter, chunk), out_shape=(j...  2.59 us

profile of v3, /device:TPU:0, one launch (start us, length us, event | category | flops | bytes accessed | tf_op | source)
XLA Modules:
  0.0 56.6 jit_solution(8753601089672051343)
XLA Ops:
  0.6 0.0 copy-start
  0.6 53.4 %transport.1 = (bf16[2,4096,128]{2,1,0:T(8,128)(2,1)S(1)}, f32[4,3,2,4,128]{4,3,2,1,0:T(4,128)}, f32[2,4,128]{2,1,0:T(4,128)S(1)}, f32[2,4,128]{2,1,0:T(4,128)S(1)}, f32[2,4,128]{2,1,0:T(4,128)S(1)}) custom-call(s32[4]{0:T(128)} %blocks_ref.3, bf16[2,4,1024,128]{3,2,1,0:T(8,128)(2,1)} %bitcast.10), custom_call_target="tpu_custom_call" | custom-call | tf_op jit(solution)/shard_map/transport/pallas_call | solution.py:265
  54.0 0.0 copy-done
  54.0 2.6 %finish.1 = (bf16[2,4096,128]{2,1,0:T(8,128)(2,1)}, f32[2,4,128]{2,1,0:T(4,128)}, f32[2,4,128]{2,1,0:T(4,128)}) custom-call(s32[4]{0:T(128)S(1)} %copy-done, bf16[2,4096,128]{2,1,0:T(8,128)(2,1)S(1)} %get-tuple-element.10.recv_ref, f32[2,4,128]{2,1,0:T(4,128)S(1)} %get-tuple-element.11.c_ref, f32[2,4,128]{2,1,0:T(4,128)S(1)} %get-tuple-element.12.s_ref, ...), custom_call_target="tpu_custom_call" | custom-call | tf_op jit(solution)/shard_map/finish/pallas_call | solution.py:293
Async XLA Ops:
  0.6 53.4 %copy-start = (s32[4]{0:T(128)S(1)}, s32[4]{0:T(128)}, u32[]{:S(2)}) copy-start(s32[4]{0:T(128)} %blocks_ref.3) | copy-start | bytes 52

commit v4 on v2

--- a/solution.py
+++ b/solution.py
@@ -24,8 +24,8 @@
     return jnp.where(me < n - 1 - me, n - 1, 0)
 
 
-def transport(n, quarter, chunk, blocks_ref, kv_ref, recv_ref, stats_ref, centers_ref, scales_ref,
-              inverse_ref, blocks, local, load_sem, blocks_sem, own_sem, send_sem, recv_sem,
+def transport(n, quarter, chunk, blocks_ref, kv_ref, recv_ref, centers_ref, scales_ref,
+              inverse_ref, length_ref, stats_ref, blocks, local, load_sem, blocks_sem, own_sem, send_sem, recv_sem,
               stat_send, stat_recv):
     kinds, users, per_dev, width = kv_ref.shape
     part = per_dev // quarter
@@ -139,6 +139,8 @@
     for u in range(users):
         length = jnp.where(user == u, blocks[u] * BLOCK, length)
 
+    length_ref[...] = length
+
     def normalise(source, k):
         center = centers_ref[k, pl.ds(user, 1), :]
         inverse = inverse_ref[k, pl.ds(user, 1), :]
@@ -172,8 +174,8 @@
                 bulk(me, s, k).wait_send()
 
 
-def finish(n, quarter, chunk, blocks_ref, recv_ref, c_ref, s_ref, i_ref, out_ref, centers_ref,
-           scales_ref, ready, out_sem, ready_sem):
+def finish(n, quarter, chunk, length_ref, recv_ref, c_ref, s_ref, i_ref, out_ref, centers_ref,
+           scales_ref, ready, out_sem, ready_sem, small_sem):
     kinds, positions, width = recv_ref.shape
     part = positions // n
     me = lax.axis_index("seq")
@@ -190,8 +192,15 @@
             for k in range(kinds):
                 place(s, k).start()
 
+    small = [
+        pltpu.make_async_copy(c_ref, centers_ref, small_sem.at[0]),
+        pltpu.make_async_copy(s_ref, scales_ref, small_sem.at[1]),
+    ]
+    for copy in small:
+        copy.start()
+
     user = me // quarter
-    length = blocks_ref[user] * BLOCK
+    length = length_ref[...]
     first = last * part * quarter + (me % quarter) * part
     steps = part // chunk
 
@@ -211,8 +220,8 @@
                 recv_ref, k, rows, first + i * chunk, length, center, inverse
             )
             late(k, i).start()
-    centers_ref[...] = c_ref[...]
-    scales_ref[...] = s_ref[...]
+    for copy in small:
+        copy.wait()
     for k in range(kinds):
         for i in range(steps):
             late(k, i).wait()
@@ -238,18 +247,19 @@
     hbm = pl.BlockSpec(memory_space=pltpu.HBM)
     chunk = min(part, CHUNK)
     small = jax.ShapeDtypeStruct((kinds, user_count, width), jnp.float32)
-    recv, _, centers, scales, inverse = pl.pallas_call(
+    recv, centers, scales, inverse, length = pl.pallas_call(
         functools.partial(transport, n, quarter, chunk),
         out_shape=(
             jax.ShapeDtypeStruct((kinds, n * part, width), jnp.bfloat16),
-            jax.ShapeDtypeStruct((n, 3, kinds, user_count, width), jnp.float32),
             small,
             small,
             small,
+            jax.ShapeDtypeStruct((1, width), jnp.int32),
         ),
         in_specs=[hbm, hbm],
         out_specs=(vmem,) * 5,
         scratch_shapes=[
+            pltpu.VMEM((n, 3, kinds, user_count, width), jnp.float32),
             pltpu.SMEM((user_count,), jnp.int32),
             pltpu.VMEM((kinds, user_count, per_dev, width), jnp.bfloat16),
             pltpu.SemaphoreType.DMA,
@@ -268,16 +278,17 @@
     out, centers, scales = pl.pallas_call(
         functools.partial(finish, n, quarter, chunk),
         out_shape=(jax.ShapeDtypeStruct((kinds, n * part, width), jnp.bfloat16), small, small),
-        in_specs=[smem, vmem, vmem, vmem, vmem],
-        out_specs=(anywhere, vmem, vmem),
+        in_specs=[vmem] * 5,
+        out_specs=(anywhere, anywhere, anywhere),
         scratch_shapes=[
             pltpu.VMEM((kinds, part, width), jnp.bfloat16),
             pltpu.SemaphoreType.DMA((n, kinds)),
             pltpu.SemaphoreType.DMA((kinds, part // chunk)),
+            pltpu.SemaphoreType.DMA((2,)),
         ],
         compiler_params=pltpu.CompilerParams(vmem_limit_bytes=GRANT),
         name="finish",
-    )(valid_blocks, recv, centers, scales, inverse)
+    )(length, recv, centers, scales, inverse)
 
     def spread(x, middle):
         x = x.reshape(kind_count, layer_dev, heads_dev, *middle, width)

time: 56.7 us -> 55 us (0.970)
  Pallas kernels: 55.9 us -> 54.2 us
    pallas_call x1, Pallas kernels: 2.59 us -> 1.48 us  [on_device(): pl.pallas_call(functools.partial(finish, n, quarter, chunk), out_shape=(j...]
    pallas_call x1, Pallas kernels: 53.3 us -> 52.7 us  [on_device(): pl.pallas_call(functools.partial(transport, n, quarter, chunk), out_shape...]
where the time goes in v4:
time: 55 us; the launch traced here: 54.9 us
  Pallas kernels  54.2 us (99%)
  between operations  0.64 us (1%)
    pallas_call x1, Pallas kernels, on_device(): pl.pallas_call(functools.partial(transport, n, quarter, chunk), out_shape...  52.7 us
    pallas_call x1, Pallas kernels, on_device(): pl.pallas_call(functools.partial(finish, n, quarter, chunk), out_shape=(j...  1.48 us

profile of v4, /device:TPU:0, one launch (start us, length us, event | category | flops | bytes accessed | tf_op | source)
XLA Modules:
  0.0 54.9 jit_solution(3724125999904151635)
XLA Ops:
  0.6 52.7 %transport.1 = (bf16[2,4096,128]{2,1,0:T(8,128)(2,1)S(1)}, f32[2,4,128]{2,1,0:T(4,128)S(1)}, f32[2,4,128]{2,1,0:T(4,128)S(1)}, f32[2,4,128]{2,1,0:T(4,128)S(1)}, s32[1,128]{1,0:T(1,128)S(1)}) custom-call(s32[4]{0:T(128)} %blocks_ref.1, bf16[2,4,1024,128]{3,2,1,0:T(8,128)(2,1)} %bitcast.10), custom_call_target="tpu_custom_call" | custom-call | tf_op jit(solution)/shard_map/transport/pallas_call | solution.py:250
  53.4 1.5 %finish.1 = (bf16[2,4096,128]{2,1,0:T(8,128)(2,1)}, f32[2,4,128]{2,1,0:T(4,128)}, f32[2,4,128]{2,1,0:T(4,128)}) custom-call(s32[1,128]{1,0:T(1,128)S(1)} %get-tuple-element.11.length_ref, bf16[2,4096,128]{2,1,0:T(8,128)(2,1)S(1)} %get-tuple-element.12.recv_ref, f32[2,4,128]{2,1,0:T(4,128)S(1)} %get-tuple-element.13.c_ref, ...), custom_call_target="tpu_custom_call" | custom-call | tf_op jit(solution)/shard_map/finish/pallas_call | solution.py:278
